TPU v7x, 256 devices: a whole 4x4x8 slice. The times are simulated.
256 devices in a mesh: freq: 16 (over z, core), tm: 16 (over y, x).
Axes of the slice: x: 4, y: 4, z: 8, core: 2. Of those that a mesh axis runs over, the one named last changes fastest.
Arguments:
- band_state: float32 [2048, 16384], P('freq', 'tm'), may hold values from -2.5 to 2.5
- lower_rows: int32 [3, 2048], replicated, may hold values from 0 to 2047, as said below
- upper_rows: int32 [3, 2048], replicated, may hold values from 0 to 2047, as said below
- delays: int32 [3, 2048], replicated, may hold values from 0 to 1024, as said below
- counts: int32 [7], replicated, may hold values from 256 to 2048, as said below
Outputs:
- dedispersed: float32 [2048, 16384], P('freq', 'tm')
Inputs may be any that keep to these rules, and one draw needn't show every extreme that they name: `counts`: entry 8 - 8 / 2^k + b is the live row count of output sub-band b of iteration k; it lies between half and all of that sub-band's 2 * 2048 / 2^(3 - k) padded rows, and in every iteration some sub-band has all its rows live. With w = 2048 / 2^(3 - k), lower_rows[k, i] is a row of input sub-band 2 * floor(i / (2 * w)) whose position in that sub-band is below its live count (all w rows are live in iteration 0). With w = 2048 / 2^(3 - k), upper_rows[k, i] is a row of input sub-band 2 * floor(i / (2 * w)) + 1 whose position in that sub-band is below its live count (all w rows are live in iteration 0). delays[k, i] is at most 2048 / 2^(3 - k), and equals it at some row in every iteration.
All inputs are finite; a program needn't handle non-finite values.
Results may differ from a plain program's by a relative error of at most 0.0003.
Values sent between devices are 32-bit elements; how exact they have to be, the bound alone decides.
A program may use at most 64 MiB of HBM per device.

v0:
```python
import jax
import jax.numpy as jnp
from jax import lax
from jax.sharding import PartitionSpec as P

DMAX = 2048
ITERS = 3


def shifted_2(block, axis, distance):
    devices = range(lax.axis_size(axis))
    route = [(i - distance, i) for i in devices if i - distance in devices]
    return lax.ppermute(block, axis, route)


def delay_columns(extended, shifts, widest):
    row_count = extended.shape[0]
    for bit_index in range(widest.bit_length()):
        stride = 1 << bit_index
        shifted = jnp.concatenate(
            [jnp.zeros((row_count, stride), extended.dtype), extended[:, :-stride]], axis=1
        )
        extended = jnp.where((shifts >> bit_index & 1)[:, None] == 1, shifted, extended)
    return extended


def live_mask(global_rows, counts, width_out, offset, bands_out):
    band_index = global_rows // width_out
    band_counts = counts[offset : offset + bands_out]
    matches = band_index[:, None] == jnp.arange(bands_out, dtype=jnp.int32)[None, :]
    live_count = jnp.sum(jnp.where(matches, band_counts[None, :], 0), axis=1)
    return global_rows % width_out < live_count


def per_device(band_state, lower_rows, upper_rows, delays, counts):
    row_count, samples = band_state.shape
    freq_index = lax.axis_index("freq")
    first_row = freq_index * row_count
    global_rows = first_row + jnp.arange(row_count, dtype=jnp.int32)
    current = band_state
    for iteration in range(ITERS):
        width_in = DMAX >> ITERS - iteration
        width_out = 2 * width_in
        bands_out = DMAX // width_out
        offset = 2**ITERS - 2 ** (ITERS - iteration)
        lower_source = lax.dynamic_slice_in_dim(lower_rows[iteration], first_row, row_count)
        upper_source = lax.dynamic_slice_in_dim(upper_rows[iteration], first_row, row_count)
        own_delays = lax.dynamic_slice_in_dim(delays[iteration], first_row, row_count)
        gathered = lax.all_gather(current, "freq", axis=0, tiled=True)
        lower_values = jnp.take(gathered, lower_source, axis=0)
        upper_values = jnp.take(gathered, upper_source, axis=0)
        rim_columns = shifted_2(upper_values[:, samples - width_in :], "tm", 1)
        extended = jnp.concatenate([rim_columns, upper_values], axis=1)
        delayed = delay_columns(extended, own_delays, width_in)[:, width_in:]
        live_rows = live_mask(global_rows, counts, width_out, offset, bands_out)
        current = jnp.where(live_rows[:, None], lower_values + delayed, jnp.zeros_like(delayed))
    return current


def solution(mesh):
    return jax.shard_map(
        per_device,
        mesh=mesh,
        in_specs=(P("freq", "tm"), P(), P(), P(), P()),
        out_specs=P("freq", "tm"),
        check_vma=False,
    )
```

profile of v0, /device:TPU:8, one launch (start us, length us, event | category | flops | bytes accessed | tf_op | source)
XLA Modules:
  0.0 244.1 jit_solution(487976752341627834)
XLA Ops:
  6.5 0.7 all-gather.4.cloned.1.call-update
  7.3 0.9 fusion.24
  8.2 0.9 fusion.23
  9.1 0.9 fusion.25
  10.1 0.7 select_reduce_fusion
  10.8 57.1 %all-gather.4.cloned.1.call-done = f32[2048,1024]{1,0:T(8,128)} async-done(((f32[128,1024]{1,0:T(8,128)}), f32[2048,1024]{1,0:T(8,128)}) %all-gather.4.cloned.1.call-update) | async-done | bytes 8388624 | tf_op jit(solution)/shard_map/all_gather | solution.py:49
  67.9 4.4 %gather_fusion.1 = f32[128,1024]{1,0:T(8,128)S(1)} fusion(f32[2048,1024]{1,0:T(8,128)} %all-gather.4.cloned.1.call-done, s32[1024]{0:T(1024)S(1)} %pad_clamp_fusion.4), kind=kCustom, calls=%fused_computation.1.clone | custom fusion | bytes 1049088 | tf_op jit(solution)/shard_map/jit(_take)/gather | solution.py:51
  72.5 3.4 %collective-permute-start = (f32[128,256]{1,0:T(8,128)S(1)}, f32[128,256]{1,0:T(8,128)S(1)}, u32[]{:S(2)}, u32[]{:S(2)}) collective-permute-start(f32[128,256]{1,0:T(8,128)S(1)} %slice.200), channel_id=1, source_target_pairs={{0,1},{1,2},{2,3},{3,4},{4,5},{5,6},{6,7},{7,8},{8,9},{9,10},{10,1... | collective-permute-start | bytes 393224 | tf_op jit(solution)/shard_map/ppermute | solution.py:13
  75.9 4.4 %gather_fusion = f32[128,1024]{1,0:T(8,128)S(1)} fusion(f32[2048,1024]{1,0:T(8,128)} %all-gather.4.cloned.1.call-done, s32[1024]{0:T(1024)S(1)} %pad_clamp_fusion.5), kind=kCustom, calls=%fused_computation.clone | custom fusion | bytes 1049088 | tf_op jit(solution)/shard_map/jit(_take)/gather | solution.py:50
  80.3 1.8 collective-permute-done
  84.2 1.0 fusion.11
  85.5 52.2 %all-gather.6.cloned.1.call-done = f32[2048,1024]{1,0:T(8,128)} async-done(((f32[128,1024]{1,0:T(8,128)}), f32[2048,1024]{1,0:T(8,128)}) %all-gather.6.cloned.1.call-update) | async-done | bytes 8388624 | tf_op jit(solution)/shard_map/all_gather | solution.py:49
  137.7 4.4 %gather_fusion.3 = f32[128,1024]{1,0:T(8,128)S(1)} fusion(f32[2048,1024]{1,0:T(8,128)} %all-gather.6.cloned.1.call-done, s32[1024]{0:T(1024)S(1)} %pad_clamp_fusion.2), kind=kCustom, calls=%fused_computation.3.clone | custom fusion | bytes 1049088 | tf_op jit(solution)/shard_map/jit(_take)/gather | solution.py:51
  142.2 3.4 %collective-permute-start.1 = (f32[128,512]{1,0:T(8,128)S(1)}, f32[128,512]{1,0:T(8,128)S(1)}, u32[]{:S(2)}, u32[]{:S(2)}) collective-permute-start(f32[128,512]{1,0:T(8,128)S(1)} %slice.212), channel_id=1, source_target_pairs={{0,1},{1,2},{2,3},{3,4},{4,5},{5,6},{6,7},{7,8},{8,9},{9,10},{10,1... | collective-permute-start | bytes 786440 | tf_op jit(solution)/shard_map/ppermute | solution.py:13
  145.7 4.4 %gather_fusion.2 = f32[128,1024]{1,0:T(8,128)S(1)} fusion(f32[2048,1024]{1,0:T(8,128)} %all-gather.6.cloned.1.call-done, s32[1024]{0:T(1024)S(1)} %pad_clamp_fusion.3), kind=kCustom, calls=%fused_computation.2.clone | custom fusion | bytes 1049088 | tf_op jit(solution)/shard_map/jit(_take)/gather | solution.py:50
  150.1 4.6 %collective-permute-done.1 = f32[128,512]{1,0:T(8,128)S(1)} collective-permute-done((f32[128,512]{1,0:T(8,128)S(1)}, f32[128,512]{1,0:T(8,128)S(1)}, u32[]{:S(2)}, u32[]{:S(2)}) %collective-permute-start.1) | collective-permute-done | bytes 262176 | tf_op jit(solution)/shard_map/ppermute | solution.py:13
  157.2 1.0 fusion.9
  158.8 51.8 %all-gather.8.cloned.1.call-done = f32[2048,1024]{1,0:T(8,128)} async-done(((f32[128,1024]{1,0:T(8,128)}), f32[2048,1024]{1,0:T(8,128)}) %all-gather.8.cloned.1.call-update) | async-done | bytes 8388624 | tf_op jit(solution)/shard_map/all_gather | solution.py:49
  210.6 4.4 %gather_fusion.5 = f32[128,1024]{1,0:T(8,128)S(1)} fusion(f32[2048,1024]{1,0:T(8,128)} %all-gather.8.cloned.1.call-done, s32[1024]{0:T(1024)S(1)} %pad_clamp_fusion), kind=kCustom, calls=%fused_computation.5.clone | custom fusion | bytes 1049088 | tf_op jit(solution)/shard_map/jit(_take)/gather | solution.py:51
  215.2 3.4 %collective-permute-start.2 = (f32[128,1024]{1,0:T(8,128)S(1)}, f32[128,1024]{1,0:T(8,128)S(1)}, u32[]{:S(2)}, u32[]{:S(2)}) collective-permute-start(f32[128,1024]{1,0:T(8,128)S(1)} %broadcast_select_fusion), channel_id=1, source_target_pairs={{0,1},{1,2},{2,3},{3,4},{4,5},{5,6},{6,7},{7,8},{8,9},{9,10},{10,1... | collective-permute-start | bytes 1572872 | tf_op jit(solution)/shard_map/ppermute | solution.py:13
  218.6 0.6 fusion.13
  219.3 4.4 %gather_fusion.4 = f32[128,1024]{1,0:T(8,128)S(1)} fusion(f32[2048,1024]{1,0:T(8,128)} %all-gather.8.cloned.1.call-done, s32[1024]{0:T(1024)S(1)} %pad_clamp_fusion.1), kind=kCustom, calls=%fused_computation.4.clone | custom fusion | bytes 1049088 | tf_op jit(solution)/shard_map/jit(_take)/gather | solution.py:50
  223.7 9.5 %collective-permute-done.2 = f32[128,1024]{1,0:T(8,128)S(1)} collective-permute-done((f32[128,1024]{1,0:T(8,128)S(1)}, f32[128,1024]{1,0:T(8,128)S(1)}, u32[]{:S(2)}, u32[]{:S(2)}) %collective-permute-start.2) | collective-permute-done | bytes 524320 | tf_op jit(solution)/shard_map/ppermute | solution.py:13
  236.6 1.0 fusion.7
  (73 shorter events, 9.1 us)
Async XLA Ops:
  6.5 61.4 %all-gather.4.cloned.1.call-start = ((), (), s32[]{:S(2)}) async-start(), calls=%async_computation | async-start | bytes 8912896 | tf_op jit(solution)/shard_map/all_gather | solution.py:49
  7.3 130.4 %all-gather.6.cloned.1.call-start = ((), (), s32[]{:S(2)}) async-start(), calls=%async_computation.1 | async-start | bytes 8912896 | tf_op jit(solution)/shard_map/all_gather | solution.py:49
  72.5 9.6 %collective-permute-start = (f32[128,256]{1,0:T(8,128)S(1)}, f32[128,256]{1,0:T(8,128)S(1)}, u32[]{:S(2)}, u32[]{:S(2)}) collective-permute-start(f32[128,256]{1,0:T(8,128)S(1)} %slice.200), channel_id=1, source_target_pairs={{0,1},{1,2},{2,3},{3,4},{4,5},{5,6},{6,7},{7,8},{8,9},{9,10},{10,1... | collective-permute-start | bytes 393224 | tf_op jit(solution)/shard_map/ppermute | solution.py:13
  82.7 2.6 %copy-start = (s32[7]{0:T(128)S(1)}, s32[7]{0:T(128)}, u32[]{:S(2)}) copy-start(s32[7]{0:T(128)} %param.11) | copy-start | bytes 88
  85.2 125.4 %all-gather.8.cloned.1.call-start = ((), (), s32[]{:S(2)}) async-start(), calls=%async_computation.2 | async-start | bytes 8912896 | tf_op jit(solution)/shard_map/all_gather | solution.py:49
  142.2 12.5 %collective-permute-start.1 = (f32[128,512]{1,0:T(8,128)S(1)}, f32[128,512]{1,0:T(8,128)S(1)}, u32[]{:S(2)}, u32[]{:S(2)}) collective-permute-start(f32[128,512]{1,0:T(8,128)S(1)} %slice.212), channel_id=1, source_target_pairs={{0,1},{1,2},{2,3},{3,4},{4,5},{5,6},{6,7},{7,8},{8,9},{9,10},{10,1... | collective-permute-start | bytes 786440 | tf_op jit(solution)/shard_map/ppermute | solution.py:13
  215.2 18.1 %collective-permute-start.2 = (f32[128,1024]{1,0:T(8,128)S(1)}, f32[128,1024]{1,0:T(8,128)S(1)}, u32[]{:S(2)}, u32[]{:S(2)}) collective-permute-start(f32[128,1024]{1,0:T(8,128)S(1)} %broadcast_select_fusion), channel_id=1, source_target_pairs={{0,1},{1,2},{2,3},{3,4},{4,5},{5,6},{6,7},{7,8},{8,9},{9,10},{10,1... | collective-permute-start | bytes 1572872 | tf_op jit(solution)/shard_map/ppermute | solution.py:13
Sparse Core Ops, SparseCore 0:
  9.2 58.7 all-gather.3
  85.3 52.3 all-gather.5
  158.3 52.2 all-gather.7
where the time goes:
time: 245 us; the launch traced here: 244 us
  waiting for transfers between devices  178 us (73%)
  local copies, waits for them, and re-layouts  30.4 us (12%)
  between operations  13.6 us (6%)
  other arithmetic  12.1 us (5%)
  starting transfers between devices  10.2 us (4%)
    all_gather x3, waiting for transfers between devices, per_device(): gathered = lax.all_gather(current, 'freq', axis=0, tiled=True)  161 us
    ppermute x3, waiting for transfers between devices, shifted_2(): return lax.ppermute(block, axis, route)  15.9 us
    gather x3, local copies, waits for them, and re-layouts, per_device(): lower_values = jnp.take(gathered, lower_source, axis=0)  13.3 us
    gather x3, local copies, waits for them, and re-layouts, per_device(): upper_values = jnp.take(gathered, upper_source, axis=0)  13.3 us
    ppermute x3, starting transfers between devices, shifted_2(): return lax.ppermute(block, axis, route)  10.1 us
    select_n x27, other arithmetic, delay_columns(): jnp.where((shifts >> bit_index & 1)[:, None] == 1, shifted, extended)  7.11 us
  transfers between devices with their start and end apart: 6, of which 6 were waited for; matrix products, arithmetic and copies ran while one was open for 8% of the time, Pallas kernels for 0%

commit v1 on v0

--- a/solution.py
+++ b/solution.py
@@ -5,6 +5,14 @@
 
 DMAX = 2048
 ITERS = 3
+
+
+def gather_from_all(shard, axis, dim):
+    peers = lax.axis_size(axis)
+    repeats = [peers if d == dim else 1 for d in range(shard.ndim)]
+    return lax.all_to_all(
+        jnp.tile(shard, repeats), axis, split_axis=dim, concat_axis=dim, tiled=True
+    )
 
 
 def shifted_2(block, axis, distance):
@@ -46,7 +54,7 @@
         lower_source = lax.dynamic_slice_in_dim(lower_rows[iteration], first_row, row_count)
         upper_source = lax.dynamic_slice_in_dim(upper_rows[iteration], first_row, row_count)
         own_delays = lax.dynamic_slice_in_dim(delays[iteration], first_row, row_count)
-        gathered = lax.all_gather(current, "freq", axis=0, tiled=True)
+        gathered = gather_from_all(current, "freq", 0)
         lower_values = jnp.take(gathered, lower_source, axis=0)
         upper_values = jnp.take(gathered, upper_source, axis=0)
         rim_columns = shifted_2(upper_values[:, samples - width_in :], "tm", 1)

time: 245 us -> 647 us (2.64)
  waiting for transfers between devices: 178 us -> 568 us
  starting transfers between devices: 10.2 us -> 26.5 us
  between operations: 13.6 us -> 0.55 us
  local copies, waits for them, and re-layouts: 30.4 us -> 41.7 us
    all_to_all x0 -> x3, waiting for transfers between devices: none -> 552 us  [gather_from_all(): lax.all_to_all(jnp.tile(shard, repeats), axis, split_axis=dim, concat_axi...]
    all_gather x3 -> x0, waiting for transfers between devices: 161 us -> none  [per_device(): gathered = lax.all_gather(current, 'freq', axis=0, tiled=True)]
    all_to_all x0 -> x3, starting transfers between devices: none -> 19.1 us  [gather_from_all(): lax.all_to_all(jnp.tile(shard, repeats), axis, split_axis=dim, concat_axi...]
    another operation x0 -> x3, local copies, waits for them, and re-layouts: none -> 13.9 us  [gather_from_all(): jnp.tile(shard, repeats)]
  transfers between devices with their start and end apart: 6 -> 6, of which waited for: 6 -> 6; matrix products, arithmetic and copies ran while one was open for 8% -> 2% of each run, Pallas kernels for 0% -> 0%
where the time goes in v1:
time: 647 us
  waiting for transfers between devices  568 us (88%)
  local copies, waits for them, and re-layouts  41.7 us (6%)
  starting transfers between devices  26.5 us (4%)
  other arithmetic  9.88 us (2%)
    all_to_all x3, waiting for transfers between devices, gather_from_all(): lax.all_to_all(jnp.tile(shard, repeats), axis, split_axis=dim, concat_axi...  552 us
    all_to_all x3, starting transfers between devices, gather_from_all(): lax.all_to_all(jnp.tile(shard, repeats), axis, split_axis=dim, concat_axi...  19.1 us
    ppermute x3, waiting for transfers between devices, shifted_2(): return lax.ppermute(block, axis, route)  16.6 us
    another operation x3, local copies, waits for them, and re-layouts, gather_from_all(): jnp.tile(shard, repeats)  13.9 us
    gather x3, local copies, waits for them, and re-layouts, per_device(): lower_values = jnp.take(gathered, lower_source, axis=0)  13.3 us
    gather x3, local copies, waits for them, and re-layouts, per_device(): upper_values = jnp.take(gathered, upper_source, axis=0)  13.3 us
  transfers between devices with their start and end apart: 6, of which 6 were waited for; matrix products, arithmetic and copies ran while one was open for 2% of the time, Pallas kernels for 0%

profile of v1, /device:TPU:8, one launch (start us, length us, event | category | flops | bytes accessed | tf_op | source)
XLA Modules:
  0.0 646.7 jit_solution(9696261683808120875)
XLA Ops:
  0.0 5.3 tile.6
  5.3 8.8 %all-to-all-start = ((f32[16,128,1024]{2,1,0:T(8,128)}), f32[16,128,1024]{2,1,0:T(8,128)}, u32[]{:S(2)}, u32[]{:S(2)}) async-start(f32[16,128,1024]{2,1,0:T(8,128)} %tile.6), calls=%async_computation | async-start | bytes 16777216 | tf_op jit(solution)/shard_map/all_to_all | solution.py:13
  14.4 183.9 %all-to-all-done = f32[16,128,1024]{2,1,0:T(8,128)} async-done(((f32[16,128,1024]{2,1,0:T(8,128)}), f32[16,128,1024]{2,1,0:T(8,128)}, u32[]{:S(2)}, u32[]{:S(2)}) %all-to-all-start) | async-done | bytes 8388640 | tf_op jit(solution)/shard_map/all_to_all | solution.py:13
  198.3 4.4 gather_fusion.1
  202.9 3.4 collective-permute-start
  206.3 4.4 gather_fusion
  210.8 1.1 collective-permute-done
  214.1 4.3 tile.7
  218.4 5.2 all-to-all-start.1
  223.8 184.0 %all-to-all-done.1 = f32[16,128,1024]{2,1,0:T(8,128)} async-done(((f32[16,128,1024]{2,1,0:T(8,128)}), f32[16,128,1024]{2,1,0:T(8,128)}, u32[]{:S(2)}, u32[]{:S(2)}) %all-to-all-start.1) | async-done | bytes 8388640 | tf_op jit(solution)/shard_map/all_to_all | solution.py:13
  407.8 4.4 gather_fusion.3
  412.3 1.9 collective-permute-start.1
  414.3 4.4 gather_fusion.2
  418.8 5.3 collective-permute-done.1
  426.8 4.3 tile.8
  431.1 5.2 all-to-all-start.2
  436.3 0.6 slice.141
  436.9 183.6 %all-to-all-done.2 = f32[16,128,1024]{2,1,0:T(8,128)} async-done(((f32[16,128,1024]{2,1,0:T(8,128)}), f32[16,128,1024]{2,1,0:T(8,128)}, u32[]{:S(2)}, u32[]{:S(2)}) %all-to-all-start.2) | async-done | bytes 8388640 | tf_op jit(solution)/shard_map/all_to_all | solution.py:13
  620.5 4.4 gather_fusion.5
  625.0 2.1 collective-permute-start.2
  627.1 0.7 fusion.13
  627.9 4.4 gather_fusion.4
  632.3 10.1 %collective-permute-done.2 = f32[128,1024]{1,0:T(8,128)S(1)} collective-permute-done((f32[128,1024]{1,0:T(8,128)S(1)}, f32[128,1024]{1,0:T(8,128)S(1)}, u32[]{:S(2)}, u32[]{:S(2)}) %collective-permute-start.2) | collective-permute-done | bytes 524320 | tf_op jit(solution)/shard_map/ppermute | solution.py:21
  645.8 1.0 fusion.7
  (78 shorter events, 8.9 us)
Async XLA Ops:
  5.3 8.8 %copy-start = (s32[3,2048]{1,0:T(4,128)S(1)}, s32[3,2048]{1,0:T(4,128)}, u32[]{:S(2)}) copy-start(s32[3,2048]{1,0:T(4,128)} %param.10) | copy-start | bytes 73732
  5.3 8.9 %copy-start.1 = (s32[3,2048]{1,0:T(4,128)S(1)}, s32[3,2048]{1,0:T(4,128)}, u32[]{:S(2)}) copy-start(s32[3,2048]{1,0:T(4,128)} %param.8) | copy-start | bytes 73732
  5.3 8.9 %copy-start.2 = (s32[3,2048]{1,0:T(4,128)S(1)}, s32[3,2048]{1,0:T(4,128)}, u32[]{:S(2)}) copy-start(s32[3,2048]{1,0:T(4,128)} %param.9) | copy-start | bytes 73732
  5.3 9.0 %copy-start.3 = (s32[7]{0:T(128)S(1)}, s32[7]{0:T(128)}, u32[]{:S(2)}) copy-start(s32[7]{0:T(128)} %param.11) | copy-start | bytes 88
  5.3 193.0 %all-to-all-start = ((f32[16,128,1024]{2,1,0:T(8,128)}), f32[16,128,1024]{2,1,0:T(8,128)}, u32[]{:S(2)}, u32[]{:S(2)}) async-start(f32[16,128,1024]{2,1,0:T(8,128)} %tile.6), calls=%async_computation | async-start | bytes 16777216 | tf_op jit(solution)/shard_map/all_to_all | solution.py:13
  202.9 9.0 %collective-permute-start = (f32[128,256]{1,0:T(8,128)S(1)}, f32[128,256]{1,0:T(8,128)S(1)}, u32[]{:S(2)}, u32[]{:S(2)}) collective-permute-start(f32[128,256]{1,0:T(8,128)S(1)} %slice.200), channel_id=1, source_target_pairs={{0,1},{1,2},{2,3},{3,4},{4,5},{5,6},{6,7},{7,8},{8,9},{9,10},{10,1... | collective-permute-start | bytes 393224 | tf_op jit(solution)/shard_map/ppermute | solution.py:21
  218.4 189.4 %all-to-all-start.1 = ((f32[16,128,1024]{2,1,0:T(8,128)}), f32[16,128,1024]{2,1,0:T(8,128)}, u32[]{:S(2)}, u32[]{:S(2)}) async-start(f32[16,128,1024]{2,1,0:T(8,128)} %tile.7), calls=%async_computation.1 | async-start | bytes 16777216 | tf_op jit(solution)/shard_map/all_to_all | solution.py:13
  412.3 11.8 %collective-permute-start.1 = (f32[128,512]{1,0:T(8,128)S(1)}, f32[128,512]{1,0:T(8,128)S(1)}, u32[]{:S(2)}, u32[]{:S(2)}) collective-permute-start(f32[128,512]{1,0:T(8,128)S(1)} %slice.212), channel_id=1, source_target_pairs={{0,1},{1,2},{2,3},{3,4},{4,5},{5,6},{6,7},{7,8},{8,9},{9,10},{10,1... | collective-permute-start | bytes 786440 | tf_op jit(solution)/shard_map/ppermute | solution.py:21
  431.1 189.4 %all-to-all-start.2 = ((f32[16,128,1024]{2,1,0:T(8,128)}), f32[16,128,1024]{2,1,0:T(8,128)}, u32[]{:S(2)}, u32[]{:S(2)}) async-start(f32[16,128,1024]{2,1,0:T(8,128)} %tile.8), calls=%async_computation.2 | async-start | bytes 16777216 | tf_op jit(solution)/shard_map/all_to_all | solution.py:13
  625.0 17.4 %collective-permute-start.2 = (f32[128,1024]{1,0:T(8,128)S(1)}, f32[128,1024]{1,0:T(8,128)S(1)}, u32[]{:S(2)}, u32[]{:S(2)}) collective-permute-start(f32[128,1024]{1,0:T(8,128)S(1)} %broadcast_select_fusion), channel_id=1, source_target_pairs={{0,1},{1,2},{2,3},{3,4},{4,5},{5,6},{6,7},{7,8},{8,9},{9,10},{10,1... | collective-permute-start | bytes 1572872 | tf_op jit(solution)/shard_map/ppermute | solution.py:21
